TPU v7x, 32 devices: a whole 2x2x4 slice. The times are simulated.
32 devices in a mesh: row: 16 (over z, y, core), col: 2 (over x).
Axes of the slice: x: 2, y: 2, z: 4, core: 2. Of those that a mesh axis runs over, the one named last changes fastest.
Arguments:
- kernel: float32 [5120, 65536], P('row', 'col'), may hold values from -0.0234375 to 0.0234375
- slip: float32 [512, 65536], P('row', 'col'), may hold values from -6 to 6
- segment: int32 [5120], P(('row', 'col')), may hold values from 0 to 15
- prestress: float32 [5120, 512], P(('row', 'col')), may hold values from -4 to 4
- state: float32 [5120, 512], P(('row', 'col')), may hold values from 0.5 to 2
- normal_stress: float32 [5120], P(('row', 'col')), may hold values from 2 to 8
- a_table: float32 [16], replicated, may hold values from 0.5 to 1
- b_table: float32 [16], replicated, may hold values from 0.5 to 1
Outputs:
- new_rate: float32 [5120, 512], P(('row', 'col'))
- new_state: float32 [5120, 512], P(('row', 'col'))
All inputs are finite; a program needn't handle non-finite values.
Results may differ from a plain program's by a relative error of at most 0.00016.
Values sent between devices are 32-bit elements; how exact they have to be, the bound alone decides.
A program may use at most 192 MiB of HBM per device.

v0:
```python
import jax
import jax.numpy as jnp
from jax import lax
from jax.sharding import PartitionSpec as P


def block_product(kernel, piece):
    return lax.dot_general(
        kernel,
        piece,
        (((1,), (1,)), ((), ())),
        precision=lax.Precision.HIGHEST,
        preferred_element_type=jnp.float32,
    )


def friction(traction, segment, prestress, state, normal_stress, a_table, b_table):
    onehot = (segment[:, None] == jnp.arange(a_table.shape[0], dtype=jnp.int32)[None, :]).astype(
        jnp.float32
    )
    a_rows = jnp.dot(onehot, a_table, precision=lax.Precision.HIGHEST)
    b_rows = jnp.dot(onehot, b_table, precision=lax.Precision.HIGHEST)
    stress = prestress + traction
    new_rate = jnp.exp(-(b_rows / a_rows)[:, None] * jnp.log(state)) * jnp.sinh(
        stress / (a_rows * normal_stress)[:, None]
    )
    new_state = state + 0.1 * (1.0 - new_rate * state)
    return (new_rate, new_state)


def per_device(kernel, slip, segment, prestress, state, normal_stress, a_table, b_table):
    partial_value = block_product(kernel, lax.all_gather(slip, "row", axis=0, tiled=True))
    traction = lax.psum_scatter(partial_value, "col", scatter_dimension=0, tiled=True)
    return friction(traction, segment, prestress, state, normal_stress, a_table, b_table)


def solution(mesh):
    placed = (
        P("row", "col"),
        P("row", "col"),
        P(("row", "col")),
        P(("row", "col"), None),
        P(("row", "col"), None),
        P(("row", "col")),
        P(),
        P(),
    )
    return jax.shard_map(
        per_device,
        mesh=mesh,
        in_specs=placed,
        out_specs=(P(("row", "col"), None), P(("row", "col"), None)),
        check_vma=False,
    )
```

profile of v0, /device:TPU:0, one launch (start us, length us, event | category | flops | bytes accessed | tf_op | source)
XLA Modules:
  0.0 439.3 jit_solution(16396706003255895338)
XLA Ops:
  7.2 0.0 copy-start
  7.2 0.0 all-gather.2.cloned.1.call-start
  7.2 0.7 all-gather.2.cloned.1.call-update
  7.9 0.0 copy-start.4
  7.9 0.0 copy-start.5
  7.9 0.0 copy-start.3
  7.9 0.0 copy-start.1
  8.0 0.0 copy-start.2
  8.0 0.0 reduce-scatter.2.cloned.1.call-start
  8.0 330.4 %all-gather.2.cloned.1.call-done = f32[512,32768]{1,0:T(8,128)} async-done(((f32[32,32768]{1,0:T(8,128)}), f32[512,32768]{1,0:T(8,128)}) %all-gather.2.cloned.1.call-update) | async-done | bytes 67108880 | tf_op jit(solution)/shard_map/all_gather | solution.py:32
  338.4 75.5 %fusion.10 = f32[320,512]{1,0:T(8,128)} fusion(f32[320,32768]{1,0:T(8,128)} %param.8, f32[512,32768]{1,0:T(8,128)} %all-gather.2.cloned.1.call-done), kind=kOutput, calls=%fused_computation.14 | convolution fusion | flops 64424509440 | bytes 109707264 | tf_op jit(solution)/shard_map/dot_general | solution.py:8
  414.0 0.0 reduce-scatter.2.cloned.1.call-update
  414.0 0.0 copy-done
  414.0 0.0 copy-done.4
  414.0 0.2 fusion.3
  414.2 0.0 copy-done.5
  414.2 0.3 fusion.4
  414.5 0.0 copy-done.3
  414.5 0.1 divide_negate_fusion
  414.6 15.6 %reduce-scatter.2.cloned.1.call-done = f32[160,512]{1,0:T(8,128)} async-done(((f32[320,512]{1,0:T(8,128)}), f32[160,512]{1,0:T(8,128)}) %reduce-scatter.2.cloned.1.call-update) | async-done | bytes 327696 | tf_op jit(solution)/shard_map/reduce_scatter | solution.py:33
  430.2 0.0 copy-done.1
  430.2 0.0 copy-done.2
  430.2 2.3 multiply_add_fusion
Async XLA Ops:
  7.2 406.8 %copy-start = (f32[16]{0:T(128)S(1)}, f32[16]{0:T(128)}, u32[]{:S(2)}) copy-start(f32[16]{0:T(128)} %param.14) | copy-start | bytes 196
  7.2 331.2 %all-gather.2.cloned.1.call-start = ((), (), s32[]{:S(2)}) async-start(), calls=%async_computation.1 | async-start | bytes 71303168 | tf_op jit(solution)/shard_map/all_gather | solution.py:32
  7.9 406.1 %copy-start.4 = (s32[160]{0:T(256)S(1)}, s32[160]{0:T(256)}, u32[]{:S(2)}) copy-start(s32[160]{0:T(256)} %param.10) | copy-start | bytes 1924
  7.9 406.3 %copy-start.5 = (f32[16]{0:T(128)S(1)}, f32[16]{0:T(128)}, u32[]{:S(2)}) copy-start(f32[16]{0:T(128)} %param.15) | copy-start | bytes 196
  7.9 406.5 %copy-start.3 = (f32[160]{0:T(256)S(1)}, f32[160]{0:T(256)}, u32[]{:S(2)}) copy-start(f32[160]{0:T(256)} %param.13) | copy-start | bytes 1924
  7.9 422.2 %copy-start.1 = (f32[160,512]{1,0:T(8,128)S(1)}, f32[160,512]{1,0:T(8,128)}, u32[]{:S(2)}) copy-start(f32[160,512]{1,0:T(8,128)} %param.12) | copy-start | bytes 983044
  8.0 422.2 %copy-start.2 = (f32[160,512]{1,0:T(8,128)S(1)}, f32[160,512]{1,0:T(8,128)}, u32[]{:S(2)}) copy-start(f32[160,512]{1,0:T(8,128)} %param.11) | copy-start | bytes 983044
  8.0 422.2 %reduce-scatter.2.cloned.1.call-start = ((), (), s32[]{:S(2)}) async-start(), calls=%async_computation.2 | async-start | bytes 983040 | tf_op jit(solution)/shard_map/reduce_scatter | solution.py:33
Sparse Core Ops, SparseCore 0:
  9.6 328.7 all-gather.1
  414.1 16.0 reduce-scatter.1
where the time goes:
time: 439 us
  waiting for transfers between devices  347 us (79%)
  matrix products  76 us (17%)
  between operations  14.1 us (3%)
    all_gather x1, waiting for transfers between devices, per_device(): lax.all_gather(slip, 'row', axis=0, tiled=True)  330 us
    dot_general x1, matrix products, block_product(): lax.dot_general(kernel, piece, (((1,), (1,)), ((), ())), precision=lax.Pr...  75.5 us
    reduce_scatter x1, waiting for transfers between devices, per_device(): lax.psum_scatter(partial_value, 'col', scatter_dimension=0, tiled=True)  15.6 us
  transfers between devices with their start and end apart: 2, of which 2 were waited for; matrix products, arithmetic and copies ran while one was open for 0% of the time, Pallas kernels for 0%

commit v1 on v0

v1 whole, which is shorter than its diff:
```python
import functools

import jax
import jax.numpy as jnp
from jax import lax
from jax.experimental import pallas as pl
from jax.experimental.pallas import tpu as pltpu
from jax.sharding import PartitionSpec as P

CHUNKS = 16
MESH = pl.DeviceIdType.MESH


def split(value):
    high = value.astype(jnp.bfloat16)
    return high, (value - high.astype(jnp.float32)).astype(jnp.bfloat16)


def times(left, right):
    return lax.dot_general(
        left, right, (((1,), (1,)), ((), ())), preferred_element_type=jnp.float32
    )


def gather_product(
    rows, kernel_ref, slip_ref, total, held, slip_in, kernel_in,
    ring_send, ring_recv, pair_send, pair_recv, own_send, own_recv, slip_sem, kernel_sem,
):
    members = slip_ref.shape[0]
    width = slip_ref.shape[1] // CHUNKS
    chips = rows // 2
    rounds = chips - 1
    pairs = CHUNKS // 2
    me = lax.axis_index("row")
    core = lax.rem(me, 2)
    other = me + 1 - 2 * core
    chip = me // 2
    odd = chip % 2
    place = (1 - odd) * (chip // 2) + odd * (chips - 1 - chip // 2)

    def row_at(spot, which):
        spot = (spot + chips) % chips
        back = spot // (chips // 2)
        return ((1 - back) * 2 * spot + back * (2 * (chips - 1 - spot) + 1)) * 2 + which

    def block(ref, row, chunk):
        return ref.at[
            pl.ds(pl.multiple_of(row * members, members), members),
            pl.ds(pl.multiple_of(chunk * width, width), width),
        ]

    def own(chunk):
        return slip_ref.at[:, pl.ds(pl.multiple_of(chunk * width, width), width)]

    def chunk_of(pair, way, step):
        return 2 * pair + (step + way) % 2

    def origin(way, hops):
        return place - hops if way == 0 else place + hops

    def ring(pair, way, step):
        chunk = chunk_of(pair, way, step)
        hops = step // 2
        row = row_at(origin(way, hops), core)
        return pltpu.make_async_remote_copy(
            src_ref=own(chunk) if hops == 0 else block(held, row, chunk),
            dst_ref=block(held, row, chunk),
            send_sem=ring_send.at[way, step],
            recv_sem=ring_recv.at[pair % 2, way, step],
            device_id={"row": row_at(place + 1 if way == 0 else place - 1, core)},
            device_id_type=MESH,
        )

    def across(pair, way, step):
        chunk = chunk_of(pair, way, step)
        piece = block(held, row_at(origin(way, step // 2 + 1), core), chunk)
        return pltpu.make_async_remote_copy(
            src_ref=piece,
            dst_ref=piece,
            send_sem=pair_send.at[way, step],
            recv_sem=pair_recv.at[pair % 3, way, step],
            device_id={"row": other},
            device_id_type=MESH,
        )

    def across_own(pair, side):
        chunk = 2 * pair + side
        return pltpu.make_async_remote_copy(
            src_ref=own(chunk),
            dst_ref=block(held, me, chunk),
            send_sem=own_send.at[side],
            recv_sem=own_recv.at[pair % 3, side],
            device_id={"row": other},
            device_id_type=MESH,
        )

    def kernel_load(chunk, side):
        return pltpu.make_async_copy(
            kernel_ref.at[:, pl.ds(pl.multiple_of(chunk * width, width), width)],
            kernel_in.at[side],
            kernel_sem.at[side],
        )

    def slip_start(chunk, side):
        def place_in(row):
            return slip_in.at[side, pl.ds(pl.multiple_of(row * members, members), members)]

        pltpu.make_async_copy(own(chunk), place_in(me), slip_sem.at[side]).start()

        def one(at, carry):
            row = (me + at) % rows
            pltpu.make_async_copy(
                block(held, row, chunk), place_in(row), slip_sem.at[side]
            ).start()
            return carry

        lax.fori_loop(1, rows, one, 0)

    def slip_wait(chunk, side):
        pltpu.make_async_copy(
            held.at[:, pl.ds(pl.multiple_of(chunk * width, width), width)],
            slip_in.at[side],
            slip_sem.at[side],
        ).wait()

    depth = min(width, 512)

    def product(side):
        def one(at, carry):
            columns = pl.ds(pl.multiple_of(at * depth, depth), depth)
            k_high, k_low = split(kernel_in[side, :, columns])
            s_high, s_low = split(slip_in[side, :, columns])
            total[...] += times(k_high, s_high) + (times(k_high, s_low) + times(k_low, s_high))
            return carry

        lax.fori_loop(0, width // depth, one, 0)

    total[...] = jnp.zeros_like(total)

    def arrival(pair, way, step):
        ring(pair, way, step).wait_recv()

    def pass_across(pair, way, step):
        @pl.when(pair > 0)
        def _():
            across(pair, way, step).wait_send()

        across(pair, way, step).start()

    def travel(pair, carry):
        sending = pair < pairs
        draining = pair > 0
        for step in range(rounds):

            @pl.when(sending)
            def _():
                for way in range(2):
                    if step >= 2:
                        arrival(pair, way, step - 2)

                    @pl.when(draining)
                    def _():
                        ring(pair, way, step).wait_send()

                    ring(pair, way, step).start()
                if step < 2:

                    @pl.when(draining)
                    def _():
                        across_own(pair, step).wait_send()

                    across_own(pair, step).start()
                else:
                    for way in range(2):
                        pass_across(pair, way, step - 2)

            @pl.when(draining)
            def _():
                if step < 2:
                    for way in range(2):
                        arrival(pair - 1, way, rounds - 2 + step)
                        pass_across(pair - 1, way, rounds - 2 + step)
                if step == 0:
                    for side in range(2):
                        kernel_load(2 * pair - 2 + side, side).start()
                if step == 2:
                    for side in range(2):
                        across_own(pair - 1, side).wait_recv()
                    for way in range(2):
                        for back in range(rounds):
                            across(pair - 1, way, back).wait_recv()
                    for side in range(2):
                        slip_start(2 * pair - 2 + side, side)
                if step in (3, 5):
                    side = (step - 3) // 2
                    kernel_load(2 * pair - 2 + side, side).wait()
                    slip_wait(2 * pair - 2 + side, side)
                    product(side)

        return carry

    lax.fori_loop(0, pairs + 1, travel, 0)
    last = pairs - 1
    for way in range(2):
        for step in range(rounds):
            ring(last, way, step).wait_send()
            across(last, way, step).wait_send()
    for side in range(2):
        across_own(last, side).wait_send()


def traction_partial(rows, kernel, slip):
    targets, columns = kernel.shape
    members = slip.shape[0] * rows
    width = columns // CHUNKS
    rounds = rows // 2 - 1
    dma = pltpu.SemaphoreType.DMA
    flops = 6 * targets * members * columns
    return pl.pallas_call(
        functools.partial(gather_product, rows),
        out_shape=(
            jax.ShapeDtypeStruct((targets, members), jnp.float32),
            jax.ShapeDtypeStruct((members, columns), jnp.float32),
        ),
        in_specs=[pl.BlockSpec(memory_space=pl.ANY)] * 2,
        out_specs=(pl.BlockSpec(memory_space=pltpu.VMEM), pl.BlockSpec(memory_space=pl.ANY)),
        scratch_shapes=[
            pltpu.VMEM((2, members, width), jnp.float32),
            pltpu.VMEM((2, targets, width), jnp.float32),
            dma((2, rounds)),
            dma((2, 2, rounds)),
            dma((2, rounds)),
            dma((3, 2, rounds)),
            dma((2,)),
            dma((3, 2)),
            dma((2,)),
            dma((2,)),
        ],
        compiler_params=pltpu.CompilerParams(
            has_side_effects=True, vmem_limit_bytes=48 * 1024 * 1024
        ),
        cost_estimate=pl.CostEstimate(
            flops=flops, bytes_accessed=4 * members * columns * 4, transcendentals=0
        ),
    )(kernel, slip)[0]


def add_over_columns(partial_value, columns):
    if columns != 2:
        return lax.psum_scatter(partial_value, "col", scatter_dimension=0, tiled=True)
    half = partial_value.shape[0] // 2
    me = lax.axis_index("col")
    mine = lax.dynamic_slice_in_dim(partial_value, me * half, half, 0)
    theirs = lax.dynamic_slice_in_dim(partial_value, (1 - me) * half, half, 0)
    return mine + lax.ppermute(theirs, "col", [(0, 1), (1, 0)])


def friction(traction, segment, prestress, state, normal_stress, a_table, b_table):
    onehot = (segment[:, None] == jnp.arange(a_table.shape[0], dtype=jnp.int32)[None, :]).astype(
        jnp.float32
    )
    a_rows = jnp.dot(onehot, a_table, precision=lax.Precision.HIGHEST)
    b_rows = jnp.dot(onehot, b_table, precision=lax.Precision.HIGHEST)
    stress = prestress + traction
    new_rate = jnp.exp(-(b_rows / a_rows)[:, None] * jnp.log(state)) * jnp.sinh(
        stress / (a_rows * normal_stress)[:, None]
    )
    new_state = state + 0.1 * (1.0 - new_rate * state)
    return (new_rate, new_state)


def per_device(rows, columns, kernel, slip, segment, prestress, state, normal_stress, a_table, b_table):
    traction = add_over_columns(traction_partial(rows, kernel, slip), columns)
    return friction(traction, segment, prestress, state, normal_stress, a_table, b_table)


def solution(mesh):
    placed = (
        P("row", "col"),
        P("row", "col"),
        P(("row", "col")),
        P(("row", "col"), None),
        P(("row", "col"), None),
        P(("row", "col")),
        P(),
        P(),
    )
    return jax.shard_map(
        functools.partial(per_device, mesh.shape["row"], mesh.shape["col"]),
        mesh=mesh,
        in_specs=placed,
        out_specs=(P(("row", "col"), None), P(("row", "col"), None)),
        check_vma=False,
    )
```

time: 439 us -> 350 us (0.80)
  waiting for transfers between devices: 347 us -> 8.54 us
  Pallas kernels: 0 us -> 335 us
  matrix products: 76 us -> 0.47 us
  between operations: 14.1 us -> 0.7 us
    pallas_call x0 -> x1, Pallas kernels: none -> 335 us  [traction_partial(): pl.pallas_call(functools.partial(gather_product, rows), out_shape=(jax.Sh...]
    all_gather x1 -> x0, waiting for transfers between devices: 330 us -> none  [per_device(): lax.all_gather(slip, 'row', axis=0, tiled=True)]
    dot_general x1 -> x0, matrix products: 75.5 us -> none  [block_product(): lax.dot_general(kernel, piece, (((1,), (1,)), ((), ())), precision=lax.Pr...]
    reduce_scatter x1 -> x0, waiting for transfers between devices: 15.6 us -> none  [per_device(): lax.psum_scatter(partial_value, 'col', scatter_dimension=0, tiled=True)]
    ppermute x0 -> x1, waiting for transfers between devices: none -> 8.54 us  [add_over_columns(): return mine + lax.ppermute(theirs, 'col', [(0, 1), (1, 0)])]
  transfers between devices with their start and end apart: 2 -> 1, of which waited for: 2 -> 1; matrix products, arithmetic and copies ran while one was open for 0% -> 0% of each run, Pallas kernels for 0% -> 0%
where the time goes in v1:
time: 350 us
  Pallas kernels  335 us (96%)
  waiting for transfers between devices  8.54 us (2%)
    pallas_call x1, Pallas kernels, traction_partial(): pl.pallas_call(functools.partial(gather_product, rows), out_shape=(jax.Sh...  335 us
    ppermute x1, waiting for transfers between devices, add_over_columns(): return mine + lax.ppermute(theirs, 'col', [(0, 1), (1, 0)])  8.54 us
  transfers between devices with their start and end apart: 1, of which 1 were waited for; matrix products, arithmetic and copies ran while one was open for 0% of the time, Pallas kernels for 0%

profile of v1, /device:TPU:0, one launch (start us, length us, event | category | flops | bytes accessed | tf_op | source)
XLA Modules:
  0.0 349.8 jit_solution(4532020639833581238)
XLA Ops:
  0.6 0.0 copy-start
  0.7 0.0 copy-start.1
  0.7 2.2 copy-done.1
  2.8 0.0 copy-start.5
  2.8 0.0 copy-start.6
  2.8 0.0 copy-start.4
  2.8 0.0 copy-start.2
  2.9 0.0 copy-start.3
  2.9 334.9 %shard_map.95 = (f32[320,512]{1,0:T(8,128)S(1)}, f32[512,32768]{1,0:T(8,128)}) custom-call(f32[320,32768]{1,0:T(8,128)} %kernel_ref.1, f32[32,32768]{1,0:T(8,128)S(1)} %copy-done.1), custom_call_target="tpu_custom_call" | custom-call | flops 32212254720 | bytes 268435456 | tf_op jit(solution)/shard_map/pallas_call | solution.py:219
  337.8 1.5 collective-permute-start
  339.4 0.0 copy-done
  339.4 0.0 copy-done.5
  339.4 0.2 fusion.4
  339.6 0.0 copy-done.6
  339.6 0.3 fusion.3
  339.8 0.0 copy-done.4
  339.8 0.1 divide_negate_fusion
  339.9 8.5 %collective-permute-done = f32[160,512]{1,0:T(8,128)S(1)} collective-permute-done((f32[160,512]{1,0:T(8,128)S(1)}, f32[160,512]{1,0:T(8,128)S(1)}, u32[]{:S(2)}, u32[]{:S(2)}) %collective-permute-start) | collective-permute-done | bytes 327712 | tf_op jit(solution)/shard_map/ppermute | solution.py:255
  348.5 0.0 copy-done.2
  348.5 0.0 copy-done.3
  348.5 1.3 multiply_add_fusion
  (1 shorter events, 0.0 us)
Async XLA Ops:
  0.6 338.7 %copy-start = (f32[16]{0:T(128)S(1)}, f32[16]{0:T(128)}, u32[]{:S(2)}) copy-start(f32[16]{0:T(128)} %param.15) | copy-start | bytes 196
  0.7 2.2 copy-start.1
  2.8 336.5 %copy-start.5 = (s32[160]{0:T(256)S(1)}, s32[160]{0:T(256)}, u32[]{:S(2)}) copy-start(s32[160]{0:T(256)} %param.10) | copy-start | bytes 1924
  2.8 336.7 %copy-start.6 = (f32[16]{0:T(128)S(1)}, f32[16]{0:T(128)}, u32[]{:S(2)}) copy-start(f32[16]{0:T(128)} %param.14) | copy-start | bytes 196
  2.8 337.0 %copy-start.4 = (f32[160]{0:T(256)S(1)}, f32[160]{0:T(256)}, u32[]{:S(2)}) copy-start(f32[160]{0:T(256)} %param.13) | copy-start | bytes 1924
  2.8 345.6 %copy-start.2 = (f32[160,512]{1,0:T(8,128)S(1)}, f32[160,512]{1,0:T(8,128)}, u32[]{:S(2)}) copy-start(f32[160,512]{1,0:T(8,128)} %param.12) | copy-start | bytes 983044
  2.9 345.6 %copy-start.3 = (f32[160,512]{1,0:T(8,128)S(1)}, f32[160,512]{1,0:T(8,128)}, u32[]{:S(2)}) copy-start(f32[160,512]{1,0:T(8,128)} %param.11) | copy-start | bytes 983044
  337.8 10.6 %collective-permute-start = (f32[160,512]{1,0:T(8,128)S(1)}, f32[160,512]{1,0:T(8,128)S(1)}, u32[]{:S(2)}, u32[]{:S(2)}) collective-permute-start(f32[160,512]{1,0:T(8,128)S(1)} %constant_dynamic-slice_fusion), channel_id=1, source_target_pairs={{0,1},{1,0},{2,3},{3,2},{4,5},{5,4},{6,7},{7,6},{8,9},{9,8},{10,11... | collective-permute-start | bytes 983048 | tf_op jit(solution)/shard_map/ppermute | solution.py:255
